TPU v7x, 32 devices: a whole 2x2x4 slice. The times are simulated.
32 devices in a mesh: pipe: 4 (over x, core), vocab: 8 (over z, y).
Axes of the slice: x: 2, y: 2, z: 4, core: 2. Of those that a mesh axis runs over, the one named last changes fastest.
Arguments:
- hidden: bfloat16 [4, 128, 4096], P('pipe'), may hold values from -60 to 60
- norm_gain: float32 [4096], replicated, may hold values from 0.5 to 1.5
- out_weight: bfloat16 [128256, 4096], P(('pipe', 'vocab')), may hold values from -4 to 4
- targets: int32 [4, 128], P('pipe'), may hold values from 0 to 128255
- loss_mask: int32 [4, 128], P('pipe'), may hold values from 0 to 1, as said below
- slot_position: int32 [4, 128], P('pipe'), may hold values from 0 to 127, each once within a row
- counts: int32 [4], replicated, may hold values from 1 to 128, 320 in all
- loss_scale: float32 [], replicated, may hold values from 4096 to 32768
Outputs:
- loss: float32 [], replicated
- grad_hidden: bfloat16 [4, 128, 4096], P('pipe')
Inputs may be any that keep to these rules, and one draw needn't show every extreme that they name: The 4 counts sum to exactly 320, and one of them equals 128. Each row of slot_position holds every number of 0 to 127 once. Each row of loss_mask holds at least 64 ones.
All inputs are finite; a program needn't handle non-finite values.
Results may differ from a plain program's by a relative error of at most 0.0034.
Values may be sent and summed in bfloat16 or wider, within the bound.
A program may use at most 128 MiB of HBM per device.

v0:
```python
import functools
import jax
import jax.numpy as jnp
from jax import lax
from jax.experimental import pallas as pl
from jax.experimental.pallas import tpu as pltpu
from jax.sharding import PartitionSpec as P

EPSILON = 1e-05
MESH = pl.DeviceIdType.MESH
F32 = jnp.float32
BF16 = jnp.bfloat16
VMEM = pl.BlockSpec(memory_space=pltpu.VMEM)


def rms_scale(values, norm_gain):
    mean_square = jnp.mean(values * values, axis=-1, keepdims=True)
    return values * lax.rsqrt(mean_square + EPSILON) * norm_gain


def pull_rows(rows, norm_gain, cotangent):
    pullback = jax.vjp(lambda values: rms_scale(values, norm_gain), rows)[1]
    return pullback(cotangent)[0].astype(BF16)


def place(ny):
    p, v = lax.axis_index("pipe"), lax.axis_index("vocab")
    return p // 2, p % 2, v % ny, v // ny


def greet(targets):
    barrier = pltpu.get_barrier_semaphore()
    for target in targets:
        pl.semaphore_signal(barrier, inc=1, device_id=target, device_id_type=MESH)
    pl.semaphore_wait(barrier, len(targets))


def remote(src, dst, send, recv, target):
    return pltpu.make_async_remote_copy(
        src_ref=src, dst_ref=dst, send_sem=send, recv_sem=recv,
        device_id=target, device_id_type=MESH,
    )


def gather_kernel(ny, chunks, own, ints, out, oints, sems_s, sems_r, own_s, own_r, int_s, int_r):
    x, core, y, z = place(ny)
    p, v = x * 2 + core, z * ny + y
    mate = (x * 2 + (1 - core), v)
    across = ((1 - x) * 2 + core, v)
    diag = ((1 - x) * 2 + (1 - core), v)
    beside = (p, z * ny + (1 - y))
    greet([mate, across, diag, beside])
    far = (1 - x) * 2 + core
    started = []
    first = []
    for c in range(chunks):
        cp = remote(own.at[y, c], out.at[p, y, c], sems_s.at[0, c], sems_r.at[0, c], across)
        cp.start()
        first.append(cp)
    for j, target in enumerate((mate, across, diag)):
        cp = remote(ints, oints.at[p], int_s.at[j], int_r.at[j], target)
        cp.start()
        started.append(cp)
    cp = remote(own, out.at[p], own_s, own_r, mate)
    cp.start()
    started.append(cp)
    oints[p] = ints[...]
    out[p] = own[...]
    second = []
    for c in range(chunks):
        first[c].wait_recv()
        cy = remote(out.at[far, y, c], out.at[far, y, c], sems_s.at[1, c], sems_r.at[1, c], beside)
        cy.start()
        cm = remote(out.at[far, y, c], out.at[far, y, c], sems_s.at[2, c], sems_r.at[2, c], mate)
        cm.start()
        second.append(cy)
        started.append(cm)
    for c in range(chunks):
        second[c].wait_recv()
        cm = remote(out.at[far, 1 - y, c], out.at[far, 1 - y, c], sems_s.at[3, c], sems_r.at[3, c], mate)
        cm.start()
        started.append(cm)
    for cp in started:
        cp.wait_recv()
    for cp in first + second + started:
        cp.wait_send()


def gather(own, ints, pipe, ny, chunks):
    rows, width = own.shape
    part = rows // (2 * chunks)
    out, oints = pl.pallas_call(
        functools.partial(gather_kernel, ny, chunks),
        out_shape=(
            jax.ShapeDtypeStruct((pipe, 2, chunks, part, width), BF16),
            jax.ShapeDtypeStruct((pipe,) + ints.shape, jnp.int32),
        ),
        in_specs=[VMEM, VMEM],
        out_specs=(VMEM, VMEM),
        scratch_shapes=[
            pltpu.SemaphoreType.DMA((4, chunks)),
            pltpu.SemaphoreType.DMA((4, chunks)),
            pltpu.SemaphoreType.DMA,
            pltpu.SemaphoreType.DMA,
            pltpu.SemaphoreType.DMA((3,)),
            pltpu.SemaphoreType.DMA((3,)),
        ],
        compiler_params=pltpu.CompilerParams(
            collective_id=0, has_side_effects=True, vmem_limit_bytes=24 * 2**20
        ),
    )(own.reshape(2, chunks, part, width), ints)
    return out.reshape(pipe * rows, width), oints


def stats_kernel(pipe, vocab, st, out, box, send, recv):
    p, v = lax.axis_index("pipe"), lax.axis_index("vocab")
    peers = []
    for dp in range(pipe):
        for dv in range(vocab):
            if dp or dv:
                peers.append((lax.rem(p + dp, pipe), lax.rem(v + dv, vocab)))
    greet(peers)
    copies = []
    for j, target in enumerate(peers):
        cp = remote(st, box.at[j], send.at[j], recv.at[j], target)
        cp.start()
        copies.append(cp)
    for cp in copies:
        cp.wait_recv()
    n = st.shape[1]
    own_top = st[0]
    tops = box[:, 0]
    top = jnp.maximum(own_top, jnp.max(tops, axis=0))
    total = st[1] * jnp.exp(own_top - top) + jnp.sum(
        box[:, 1] * jnp.exp(tops - top[None]), axis=0
    )
    out[0] = top + jnp.log(total)
    out[1] = st[2] + jnp.sum(box[:, 2], axis=0)
    for cp in copies:
        cp.wait_send()


def combine_stats(top, total, target, pipe, vocab):
    rows = top.shape[0]
    st = jnp.stack([top, total, target]).reshape(3, rows // 128, 128)
    n = pipe * vocab - 1
    out = pl.pallas_call(
        functools.partial(stats_kernel, pipe, vocab),
        out_shape=jax.ShapeDtypeStruct((2, rows // 128, 128), F32),
        in_specs=[VMEM],
        out_specs=VMEM,
        scratch_shapes=[
            pltpu.VMEM((n,) + st.shape, F32),
            pltpu.SemaphoreType.DMA((n,)),
            pltpu.SemaphoreType.DMA((n,)),
        ],
        compiler_params=pltpu.CompilerParams(collective_id=1, has_side_effects=True),
    )(st)
    return out[0].reshape(rows), out[1].reshape(rows)


def reduce_kernel(ny, nz, g, h, gain, out, ra, sb1, sb2, rb1, rb2, sc1, sc2, rc1, rc2,
                  u, sd, rd, s_a, r_a, s_b, r_b, s_c, r_c, s_d, r_d, s_e, r_e, s_f, r_f):
    x, core, y, z = place(ny)
    p, v = x * 2 + core, z * ny + y
    half = g.shape[-1] // 2
    lo, hi = pl.ds(0, half), pl.ds(half, half)
    mate = (x * 2 + (1 - core), v)
    across = ((1 - x) * 2 + core, v)
    beside = (p, z * ny + (1 - y))
    along = [(p, lax.rem(z + d, nz) * ny + y) for d in range(1, nz)]
    greet([mate, across, beside] + along)
    copies = []

    def go(src, dst, send, recv, target):
        cp = remote(src, dst, send, recv, target)
        cp.start()
        copies.append(cp)
        return cp

    order = ((1 - x, 1 - y), (1 - x, y), (x, 1 - y), (x, y))
    pa = [go(g.at[a, 1 - core, b], ra.at[a, b], s_a.at[j], r_a.at[j], mate)
          for j, (a, b) in enumerate(order)]

    def fill(dst, i, a, b, cols):
        def one(k, carry):
            dst[i, k] = (g[a, core, b, k, :, cols] + ra[a, b, k, :, cols]).astype(BF16)
            return carry
        lax.fori_loop(0, nz, one, 0)

    pa[0].wait_recv()
    fill(sb1, 1 - y, 1 - x, 1 - y, lo)
    b10 = go(sb1.at[1 - y], rb1.at[1 - y], s_b.at[0], r_b.at[0], across)
    fill(sb2, 1 - x, 1 - x, 1 - y, hi)
    b20 = go(sb2.at[1 - x], rb2.at[1 - x], s_b.at[1], r_b.at[1], beside)
    pa[1].wait_recv()
    fill(sb1, y, 1 - x, y, lo)
    b11 = go(sb1.at[y], rb1.at[y], s_b.at[2], r_b.at[2], across)
    pa[2].wait_recv()
    fill(sb2, x, x, 1 - y, hi)
    b21 = go(sb2.at[x], rb2.at[x], s_b.at[3], r_b.at[3], beside)
    pa[3].wait_recv()

    b10.wait_recv()

    def fc1(k, carry):
        sc1[k] = (g[x, core, 1 - y, k, :, lo] + ra[x, 1 - y, k, :, lo]
                  + rb1[1 - y, k].astype(F32)).astype(BF16)
        return carry
    lax.fori_loop(0, nz, fc1, 0)
    b20.wait_recv()

    def fc2(k, carry):
        sc2[k] = (g[1 - x, core, y, k, :, hi] + ra[1 - x, y, k, :, hi]
                  + rb2[1 - x, k].astype(F32)).astype(BF16)
        return carry
    lax.fori_loop(0, nz, fc2, 0)
    c1 = go(sc1, rc1, s_c.at[0], r_c.at[0], beside)
    c2 = go(sc2, rc2, s_c.at[1], r_c.at[1], across)
    b11.wait_recv()
    b21.wait_recv()
    c1.wait_recv()
    c2.wait_recv()

    def fu(k, carry):
        a = (g[x, core, y, k, :, lo] + ra[x, y, k, :, lo]
             + rb1[y, k].astype(F32) + rc1[k].astype(F32))
        b = (g[x, core, y, k, :, hi] + ra[x, y, k, :, hi]
             + rb2[x, k].astype(F32) + rc2[k].astype(F32))
        u[k, :, lo] = a
        u[k, :, hi] = b
        sd[k, :, lo] = a.astype(BF16)
        sd[k, :, hi] = b.astype(BF16)
        return carry
    lax.fori_loop(0, nz, fu, 0)
    pd = [go(sd.at[lax.rem(z + d, nz)], rd.at[d - 1], s_d.at[d - 1], r_d.at[d - 1], along[d - 1])
          for d in range(1, nz)]
    rows = h[y, z].astype(F32)
    scale = lax.rsqrt(jnp.mean(rows * rows, axis=-1, keepdims=True) + EPSILON)
    for cp in pd:
        cp.wait_recv()
    total = u[z]
    for d in range(1, nz):
        total = total + rd[d - 1].astype(F32)
    gg = total * gain[...]
    dot = jnp.mean(rows * gg, axis=-1, keepdims=True)
    out[y, z] = (scale * gg - (scale * scale * scale) * rows * dot).astype(BF16)

    tail = [go(out.at[y, z], out.at[y, z], s_f.at[0], r_f.at[0], beside)]
    pe = [go(out.at[y, z], out.at[y, z], s_e.at[d - 1], r_e.at[d - 1], along[d - 1])
          for d in range(1, nz)]
    for d in range(1, nz):
        pe[d - 1].wait_recv()
        zz = lax.rem(z + nz - d, nz)
        tail.append(go(out.at[y, zz], out.at[y, zz], s_f.at[d], r_f.at[d], beside))
    for cp in tail:
        cp.wait_recv()
    for cp in copies:
        cp.wait_send()


def reduce_finish(grad, rows, norm_gain, ny, nz):
    micro, width = rows.shape
    part = micro // (ny * nz)
    half = width // 2
    dma = pltpu.SemaphoreType.DMA
    out = pl.pallas_call(
        functools.partial(reduce_kernel, ny, nz),
        out_shape=jax.ShapeDtypeStruct((ny, nz, part, width), BF16),
        in_specs=[VMEM] * 3,
        out_specs=VMEM,
        scratch_shapes=[
            pltpu.VMEM((2, ny, nz, part, width), F32),
            pltpu.VMEM((ny, nz, part, half), BF16),
            pltpu.VMEM((2, nz, part, half), BF16),
            pltpu.VMEM((ny, nz, part, half), BF16),
            pltpu.VMEM((2, nz, part, half), BF16),
            pltpu.VMEM((nz, part, half), BF16),
            pltpu.VMEM((nz, part, half), BF16),
            pltpu.VMEM((nz, part, half), BF16),
            pltpu.VMEM((nz, part, half), BF16),
            pltpu.VMEM((nz, part, width), F32),
            pltpu.VMEM((nz, part, width), BF16),
            pltpu.VMEM((nz - 1, part, width), BF16),
            dma((4,)), dma((4,)), dma((4,)), dma((4,)), dma((2,)), dma((2,)),
            dma((nz - 1,)), dma((nz - 1,)), dma((nz - 1,)), dma((nz - 1,)), dma((nz,)), dma((nz,)),
        ],
        compiler_params=pltpu.CompilerParams(
            collective_id=2, has_side_effects=True, vmem_limit_bytes=40 * 2**20
        ),
    )(
        grad.reshape(2, 2, ny, nz, part, width),
        rows.reshape(ny, nz, part, width),
        norm_gain.reshape(1, width),
    )
    return out


def body(pipe, vocab, hidden, norm_gain, out_weight, targets, loss_mask, slot_position, counts, loss_scale):
    micro_slots = hidden.shape[1]
    model_width = hidden.shape[2]
    shard_words = out_weight.shape[0]
    ny = 2
    nz = vocab // ny
    fast = pipe == 4 and vocab == ny * nz and nz <= 4 and micro_slots == 16 * vocab
    offset = lax.axis_index(("pipe", "vocab")) * shard_words
    own_rows = hidden.reshape(micro_slots, model_width).astype(F32)
    own_normed = rms_scale(own_rows, norm_gain).astype(BF16)
    own_ints = jnp.concatenate(
        [targets, loss_mask, slot_position, jnp.zeros((5, micro_slots), jnp.int32)], axis=0
    )
    if fast:
        all_normed, all_ints = gather(own_normed, own_ints, pipe, ny, 4)
    else:
        all_normed = lax.all_gather(own_normed, "pipe", axis=0, tiled=True)
        all_ints = lax.all_gather(own_ints, "pipe", axis=0)
    rows_total = all_normed.shape[0]
    all_targets, all_masks, all_positions = (
        all_ints[:, k].reshape(rows_total) for k in range(3)
    )
    count_row = jnp.broadcast_to(counts[:, None], (counts.shape[0], micro_slots)).reshape(rows_total)
    inside = all_positions < count_row
    token_weight = jnp.where(inside & (all_masks == 1), 1.0, 0.0).astype(F32)
    weight_total = jnp.sum(token_weight)
    logits = lax.dot_general(
        all_normed, out_weight, (((1,), (1,)), ((), ())), preferred_element_type=F32
    )
    is_target = (
        jnp.arange(shard_words, dtype=jnp.int32)[None, :] == (all_targets - offset)[:, None]
    )
    local_target = jnp.sum(jnp.where(is_target, logits, 0.0), axis=1)
    local_top = jnp.max(logits, axis=1)
    if fast:
        local_total = jnp.sum(jnp.exp(logits - local_top[:, None]), axis=1)
        log_total, target_logit = combine_stats(local_top, local_total, local_target, pipe, vocab)
    else:
        row_top = lax.pmax(local_top, ("pipe", "vocab"))
        local_total = jnp.sum(jnp.exp(logits - row_top[:, None]), axis=1)
        exp_total, target_logit = lax.psum((local_total, local_target), ("pipe", "vocab"))
        log_total = row_top + jnp.log(exp_total)
    loss = jnp.sum(token_weight * (log_total - target_logit)) / weight_total
    token_coef = loss_scale * token_weight / weight_total
    logit_grad = (
        (jnp.exp(logits - log_total[:, None]) - is_target.astype(F32)) * token_coef[:, None]
    ).astype(BF16)
    work_grad = jnp.dot(logit_grad, out_weight, preferred_element_type=F32)
    if fast:
        grad_out = reduce_finish(work_grad, hidden.reshape(micro_slots, model_width), norm_gain, ny, nz)
    else:
        grad_cube = work_grad.reshape(rows_total // micro_slots, micro_slots, model_width)
        micro_grad = lax.psum_scatter(grad_cube, "pipe", scatter_dimension=0, tiled=True)
        summed = lax.psum(micro_grad, "vocab")
        grad_out = pull_rows(own_rows, norm_gain, summed.reshape(micro_slots, model_width))
    return (loss, grad_out.reshape(1, micro_slots, model_width))


def solution(mesh):
    in_specs = (
        P("pipe", None, None),
        P(),
        P(("pipe", "vocab"), None),
        P("pipe", None),
        P("pipe", None),
        P("pipe", None),
        P(),
        P(),
    )
    out_specs = (P(), P("pipe", None, None))
    part = functools.partial(body, mesh.shape["pipe"], mesh.shape["vocab"])
    return jax.shard_map(part, mesh=mesh, in_specs=in_specs, out_specs=out_specs, check_vma=False)
```

profile of v0, /device:TPU:16, one launch (start us, length us, event | category | flops | bytes accessed | tf_op | source)
XLA Modules:
  0.0 151.7 jit_solution(9970715197166394369)
XLA Ops:
  1.3 1.5 %multiply_reduce_fusion = f32[128]{0:T(128)S(1)} fusion(bf16[1,128,4096]{2,1,0:T(8,128)(2,1)} %param.8), kind=kLoop, calls=%fused_computation.9 | loop fusion | flops 1572736 | bytes 1049088 | tf_op jit(solution)/shard_map/reduce_sum | solution.py:17
  2.8 0.1 pad.6.clone
  2.9 0.8 add_add_fusion.ints
  3.7 0.1 rsqrt.12
  3.7 1.6 %multiply_convert_fusion.2.own = bf16[2,4,16,4096]{3,2,1,0:T(8,128)(2,1)S(1)} fusion(bf16[2,4,16,4096]{3,2,1,0:T(8,128)(2,1)} %bitcast.30, f32[4096]{0:T(1024)} %param.9, f32[2,4,16]{2,1,0:T(4,128)S(1)} %rsqrt.12), kind=kLoop, calls=%fused_computation.8 | loop fusion | flops 2097152 | bytes 2114048 | tf_op jit(solution)/shard_map/convert_element_type | solution.py:308
  5.3 20.7 %shard_map.95 = (bf16[4,2,4,16,4096]{4,3,2,1,0:T(8,128)(2,1)S(1)}, s32[4,8,128]{2,1,0:T(8,128)S(1)}) custom-call(bf16[2,4,16,4096]{3,2,1,0:T(8,128)(2,1)S(1)} %multiply_convert_fusion.2.own, s32[8,128]{1,0:T(8,128)S(1)} %add_add_fusion.ints), custom_call_target="tpu_custom_call" | custom-call | tf_op jit(solution)/shard_map/pallas_call | solution.py:92
  26.0 0.7 compare_and_fusion
  26.7 21.4 %fusion.6 = (f32[512]{0:T(512)S(1)}, f32[512,4008]{0,1:T(8,128)S(1)}) fusion(bf16[512,4096]{1,0:T(8,128)(2,1)S(1)} %bitcast.35, bf16[4008,4096]{1,0:T(8,128)(2,1)} %param.10), kind=kOutput, calls=%fused_computation.23 | convolution fusion | flops 16812822528 | bytes 45238272 | tf_op jit(solution)/shard_map/dot_general | solution.py:325
  48.1 0.0 copy-start.2
  48.2 0.0 copy-start.3
  48.2 3.1 %copy-done.2 = f32[512,4008]{0,1:T(8,128)} copy-done((f32[512,4008]{0,1:T(8,128)}, f32[512,4008]{0,1:T(8,128)S(1)}, u32[]{:S(2)}) %copy-start.2) | copy-done | bytes 8208408
  51.3 2.2 %exponential_reduce_fusion = (f32[512]{0:T(512)S(1)}, f32[512]{0:T(512)S(1)}) fusion(f32[512,4008]{0,1:T(8,128)S(1)} %get-tuple-element.13, f32[512]{0:T(512)S(1)} %get-tuple-element.12, s32[512]{0:T(512)S(1)} %bitcast.36), kind=kLoop, calls=%fused_computation.3 | loop fusion | flops 10259456 | bytes 8216576 | tf_op jit(solution)/shard_map/reduce_sum | solution.py:334
  53.5 0.6 pad_maximum_fusion.st
  54.1 11.3 %shard_map.96 = f32[2,4,128]{2,1,0:T(4,128)} custom-call(f32[3,4,128]{2,1,0:T(4,128)} %pad_maximum_fusion.st), custom_call_target="tpu_custom_call" | custom-call | tf_op jit(solution)/shard_map/pallas_call | solution.py:147
  65.4 1.3 select_reduce_fusion.1
  68.0 0.0 copy-done.3
  68.0 0.7 multiply_divide_fusion
  68.7 0.7 slice_bitcast_fusion
  69.4 0.0 copy-start
  69.4 0.0 copy-start.1
  69.4 24.3 %fusion = f32[512,4096]{1,0:T(8,128)S(1)} fusion(bf16[4008,4096]{1,0:T(8,128)(2,1)} %param.10, f32[512,4008]{0,1:T(8,128)} %copy-done.2, f32[512]{0:T(512)S(1)} %multiply_divide_fusion, f32[512]{0:T(512)S(1)} %slice_bitcast_fusion, s32[512]{0:T(512)S(1)} %bitcast.37), kind=kOutput, calls=%fused_computation.4 | convolution fusion | flops 16823083008 | bytes 49436672 | tf_op jit(solution)/shard_map/dot_general | solution.py:346
  93.7 0.0 copy-done
  93.7 0.0 copy-done.1
  93.7 55.9 %shard_map.97 = bf16[2,4,16,4096]{3,2,1,0:T(8,128)(2,1)S(1)} custom-call(f32[2,2,2,4,16,4096]{5,4,3,2,1,0:T(8,128)S(1)} %bitcast.32, bf16[2,4,16,4096]{3,2,1,0:T(8,128)(2,1)S(1)} %bitcast.31, f32[1,4096]{1,0:T(1,128)S(1)} %bitcast.34), custom_call_target="tpu_custom_call" | custom-call | tf_op jit(solution)/shard_map/pallas_call | solution.py:267
  149.6 1.0 copy.14
  (4 shorter events, 0.0 us)
Async XLA Ops:
  48.1 3.2 %copy-start.2 = (f32[512,4008]{0,1:T(8,128)}, f32[512,4008]{0,1:T(8,128)S(1)}, u32[]{:S(2)}) copy-start(f32[512,4008]{0,1:T(8,128)S(1)} %get-tuple-element.13) | copy-start | bytes 24625156
  48.2 19.8 %copy-start.3 = (s32[4]{0:T(128)S(1)}, s32[4]{0:T(128)}, u32[]{:S(2)}) copy-start(s32[4]{0:T(128)} %param.14) | copy-start | bytes 52
  69.4 24.3 %copy-start = (bf16[1,128,4096]{2,1,0:T(8,128)(2,1)S(1)}, bf16[1,128,4096]{2,1,0:T(8,128)(2,1)}, u32[]{:S(2)}) copy-start(bf16[1,128,4096]{2,1,0:T(8,128)(2,1)} %param.8) | copy-start | bytes 3145732
  69.4 24.3 %copy-start.1 = (f32[4096]{0:T(1024)S(1)}, f32[4096]{0:T(1024)}, u32[]{:S(2)}) copy-start(f32[4096]{0:T(1024)} %param.9) | copy-start | bytes 49156
where the time goes:
time: 152 us
  Pallas kernels  87.8 us (58%)
  matrix products  45.7 us (30%)
  other arithmetic  9.37 us (6%)
  local copies, waits for them, and re-layouts  4.96 us (3%)
  between operations  3.87 us (3%)
    pallas_call x1, Pallas kernels, reduce_finish(): pl.pallas_call(functools.partial(reduce_kernel, ny, nz), out_shape=jax.Sh...  55.9 us
    dot_general x1, matrix products, body(): work_grad = jnp.dot(logit_grad, out_weight, preferred_element_type=F32)  24.3 us
    dot_general x1, matrix products, body(): lax.dot_general(all_normed, out_weight, (((1,), (1,)), ((), ())), preferr...  21.4 us
    pallas_call x1, Pallas kernels, gather(): pl.pallas_call(functools.partial(gather_kernel, ny, chunks), out_shape=(j...  20.7 us
    pallas_call x1, Pallas kernels, combine_stats(): pl.pallas_call(functools.partial(stats_kernel, pipe, vocab), out_shape=ja...  11.3 us
    unnamed x9, local copies, waits for them, and re-layouts  4.12 us

commit v1 on v0

v1 whole, which is shorter than its diff:
```python
import functools
import jax
import jax.numpy as jnp
from jax import lax
from jax.experimental import pallas as pl
from jax.experimental.pallas import tpu as pltpu
from jax.sharding import PartitionSpec as P

EPSILON = 1e-05
MESH = pl.DeviceIdType.MESH
F32 = jnp.float32
BF16 = jnp.bfloat16
VMEM = pl.BlockSpec(memory_space=pltpu.VMEM)


def rms_scale(values, norm_gain):
    mean_square = jnp.mean(values * values, axis=-1, keepdims=True)
    return values * lax.rsqrt(mean_square + EPSILON) * norm_gain


def pull_rows(rows, norm_gain, cotangent):
    pullback = jax.vjp(lambda values: rms_scale(values, norm_gain), rows)[1]
    return pullback(cotangent)[0].astype(BF16)


def place(ny):
    p, v = lax.axis_index("pipe"), lax.axis_index("vocab")
    return p // 2, p % 2, v % ny, v // ny


def greet(targets):
    barrier = pltpu.get_barrier_semaphore()
    for target in targets:
        pl.semaphore_signal(barrier, inc=1, device_id=target, device_id_type=MESH)
    pl.semaphore_wait(barrier, len(targets))


def remote(src, dst, send, recv, target):
    return pltpu.make_async_remote_copy(
        src_ref=src, dst_ref=dst, send_sem=send, recv_sem=recv,
        device_id=target, device_id_type=MESH,
    )


LIVE_SHARE = 80
F_MIN = -1e30


def flip(i, by):
    return i + by * (1 - 2 * i)


def lanes_of(col):
    rows, lanes = col.shape
    outs = []
    for b in range(0, rows, lanes):
        part = col[b:min(b + lanes, rows)]
        r = lax.broadcasted_iota(jnp.int32, part.shape, 0)
        l = lax.broadcasted_iota(jnp.int32, part.shape, 1)
        outs.append(jnp.sum(jnp.where(r == l, part, 0.0), axis=0, keepdims=True))
    return outs


def col_of(row, count):
    shape = (count, row.shape[1])
    r = lax.broadcasted_iota(jnp.int32, shape, 0)
    l = lax.broadcasted_iota(jnp.int32, shape, 1)
    return jnp.sum(jnp.where(r == l, jnp.broadcast_to(row, shape), 0.0), axis=1, keepdims=True)


def gather_kernel(ny, chunks, counts, own, ints, gain, hc, nc, meta, posn, live_out,
                  hall, oints, sel, sems_s, sems_r, own_s, own_r, int_s, int_r):
    x, core, y, z = place(ny)
    p, v = x * 2 + core, z * ny + y
    pipe, slots, width = hall.shape
    part = slots // (2 * chunks)
    mate = (x * 2 + (1 - core), v)
    across = ((1 - x) * 2 + core, v)
    diag = ((1 - x) * 2 + (1 - core), v)
    beside = (p, z * ny + (1 - y))
    greet([mate, across, diag, beside])
    far = (1 - x) * 2 + core
    started = []
    first = []

    def rows(side, c):
        return pl.ds(pl.multiple_of((side * chunks + c) * part, part), part)

    for c in range(chunks):
        cp = remote(own.at[rows(y, c)], hall.at[p, rows(y, c)], sems_s.at[0, c], sems_r.at[0, c], across)
        cp.start()
        first.append(cp)
    for j, target in enumerate((mate, across, diag)):
        cp = remote(ints, oints.at[p], int_s.at[j], int_r.at[j], target)
        cp.start()
        started.append(cp)
    cp = remote(own, hall.at[p], own_s, own_r, mate)
    cp.start()
    started.append(cp)
    oints[p] = ints[...]
    hall[p] = own[...]
    second = []
    for c in range(chunks):
        first[c].wait_recv()
        cy = remote(hall.at[far, rows(y, c)], hall.at[far, rows(y, c)], sems_s.at[1, c], sems_r.at[1, c], beside)
        cy.start()
        cm = remote(hall.at[far, rows(y, c)], hall.at[far, rows(y, c)], sems_s.at[2, c], sems_r.at[2, c], mate)
        cm.start()
        second.append(cy)
        started.append(cm)
    for c in range(chunks):
        second[c].wait_recv()
        cm = remote(hall.at[far, rows(1 - y, c)], hall.at[far, rows(1 - y, c)], sems_s.at[3, c], sems_r.at[3, c], mate)
        cm.start()
        started.append(cm)
    for cp in started:
        cp.wait_recv()

    bound = hc.shape[0]
    square = (slots, slots)
    r0 = lax.broadcasted_iota(jnp.int32, square, 0)
    l0 = lax.broadcasted_iota(jnp.int32, square, 1)
    ri = lax.broadcasted_iota(jnp.int32, (bound, slots), 0).astype(F32)
    base = jnp.zeros((1, 1), F32)
    tgt = jnp.zeros((bound, 1), F32)
    for m in range(pipe):
        inside = oints[m, 2:3, :] < counts[m]
        live = jnp.where(inside & (oints[m, 1:2, :] == 1), 1.0, 0.0).astype(F32)
        live_sq = jnp.broadcast_to(live, square)
        col_live = jnp.sum(jnp.where(r0 == l0, live_sq, 0.0), axis=1, keepdims=True)
        pos_col = jnp.sum(jnp.where(l0 < r0, live_sq, 0.0), axis=1, keepdims=True) + base
        pos_row = jnp.sum(jnp.where(r0 < l0, jnp.broadcast_to(col_live, square), 0.0), axis=0, keepdims=True) + base
        one = jnp.where((ri == jnp.broadcast_to(pos_row, ri.shape))
                        & (jnp.broadcast_to(live, ri.shape) == 1.0), 1.0, 0.0)
        sel[:, m * slots:(m + 1) * slots] = one.astype(BF16)
        tgt = tgt + jnp.sum(one * oints[m, 0:1, :].astype(F32), axis=1, keepdims=True)
        posn[m] = jnp.broadcast_to(jnp.where(col_live == 1.0, pos_col, -1.0), posn.shape[1:])
        base = base + jnp.sum(live, axis=1, keepdims=True)
    live_out[...] = jnp.broadcast_to(base, live_out.shape)
    lane = (bound, meta.shape[2])
    meta[0] = jnp.broadcast_to(tgt, lane)
    rl = lax.broadcasted_iota(jnp.int32, lane, 0).astype(F32)
    meta[1] = jnp.where(rl < jnp.broadcast_to(base, lane), 1.0, 0.0)
    meta[2] = jnp.zeros(lane, F32)
    step = 512

    def compact(c, carry):
        cols = pl.ds(pl.multiple_of(c * step, step), step)
        block = hall[:, :, cols].reshape(pipe * slots, step)
        h = jnp.dot(sel[...], block, preferred_element_type=F32)
        hc[:, cols] = h.astype(BF16)
        sq = h * h
        acc = meta[2]
        for k in range(0, step, lane[1]):
            acc = acc + sq[:, k:k + lane[1]]
        meta[2] = acc
        return carry
    lax.fori_loop(0, width // step, compact, 0)
    mean = jnp.sum(meta[2], axis=1, keepdims=True) / width
    meta[2] = jnp.broadcast_to(lax.rsqrt(mean + EPSILON), lane)

    def norm(c, carry):
        cols = pl.ds(pl.multiple_of(c * lane[1], lane[1]), lane[1])
        nc[:, cols] = (hc[:, cols].astype(F32) * meta[2] * gain[:, cols]).astype(BF16)
        return carry
    lax.fori_loop(0, width // lane[1], norm, 0)
    for cp in first + second + started:
        cp.wait_send()


def gather(hidden, ints, counts, gain, pipe, ny, chunks, bound):
    slots, width = hidden.shape
    dma = pltpu.SemaphoreType.DMA
    return pl.pallas_call(
        functools.partial(gather_kernel, ny, chunks),
        out_shape=(
            jax.ShapeDtypeStruct((bound, width), BF16),
            jax.ShapeDtypeStruct((bound, width), BF16),
            jax.ShapeDtypeStruct((3, bound, 128), F32),
            jax.ShapeDtypeStruct((pipe, slots, 128), F32),
            jax.ShapeDtypeStruct((8, 128), F32),
        ),
        in_specs=[pl.BlockSpec(memory_space=pltpu.SMEM), VMEM, VMEM, VMEM],
        out_specs=(VMEM,) * 5,
        scratch_shapes=[
            pltpu.VMEM((pipe, slots, width), BF16),
            pltpu.VMEM((pipe,) + ints.shape, jnp.int32),
            pltpu.VMEM((bound, pipe * slots), BF16),
            dma((4, chunks)), dma((4, chunks)), dma, dma, dma((3,)), dma((3,)),
        ],
        compiler_params=pltpu.CompilerParams(
            collective_id=0, has_side_effects=True, vmem_limit_bytes=24 * 2**20
        ),
    )(counts, hidden, ints, gain)


def head_kernel(pipe, vocab, ny, words, scale_ref, weight, nc, hc, meta, posn, live, gain,
                out, loss, wv, lg, gb, mx, tg, st, box, st2, box2, ms, ob, mr, sb, rb, own, zs, zr, ag,
                w_sem, st_s, st_r, s2_s, s2_r, m_s, m_r, x_s, x_r, z_s, z_r, az_s, az_r,
                ax_s, ax_r, am_s, am_r):
    x, core, y, z = place(ny)
    p, v = x * 2 + core, z * ny + y
    nz = vocab // ny
    rows, width = nc.shape
    padded = wv.shape[0]
    tile = 512
    tiles = padded // tile
    rest = words - (tiles - 1) * tile
    lane = (rows, 128)
    offset = (p * vocab + v) * words

    def load(t):
        size = tile if t < tiles - 1 else rest
        return pltpu.make_async_copy(
            weight.at[pl.ds(t * tile, size)], wv.at[pl.ds(t * tile, size)], w_sem.at[t])

    for t in range(tiles - 1):
        load(t).start()
    edge = words // 16 * 16
    wv[edge:, :] = jnp.zeros((padded - edge, width), BF16)
    load(tiles - 1).start()

    peers = []
    for dp in range(pipe):
        for dv in range(vocab):
            if dp or dv:
                peers.append((lax.rem(p + dp, pipe), lax.rem(v + dv, vocab)))
    greet(peers)
    copies = []

    def go(src, dst, send, recv, target):
        cp = remote(src, dst, send, recv, target)
        cp.start()
        copies.append(cp)
        return cp

    mx[...] = jnp.full(lane, F_MIN, F32)
    tg[...] = jnp.zeros(lane, F32)

    def forward(t, carry):
        @pl.when(t < tiles - 1)
        def _():
            pltpu.make_async_copy(
                weight.at[pl.ds(pl.multiple_of(t * tile, tile), tile)],
                wv.at[pl.ds(pl.multiple_of(t * tile, tile), tile)], w_sem.at[t]).wait()

        @pl.when(t == tiles - 1)
        def _():
            load(tiles - 1).wait()
        wt = wv[pl.ds(pl.multiple_of(t * tile, tile), tile), :]
        logit = lax.dot_general(nc[...], wt, (((1,), (1,)), ((), ())), preferred_element_type=F32)
        col = lax.broadcasted_iota(jnp.int32, (1, 128), 1)
        top, hit = mx[...], tg[...]
        want = meta[0] - (offset + t * tile).astype(F32)
        for k in range(tile // 128):
            here = col + k * 128
            part = jnp.where(here + t * tile < words, logit[:, k * 128:(k + 1) * 128], F_MIN)
            lg[:, pl.ds(pl.multiple_of(t * tile + k * 128, 128), 128)] = part
            top = jnp.maximum(top, part)
            hit = hit + jnp.where((want == here.astype(F32)) & (part > F_MIN), part, 0.0)
        mx[...] = top
        tg[...] = hit
        return carry
    lax.fori_loop(0, tiles, forward, 0)

    top = jnp.max(mx[...], axis=1, keepdims=True)
    hit = jnp.sum(tg[...], axis=1, keepdims=True)
    mx[...] = jnp.broadcast_to(top, lane)
    tg[...] = jnp.zeros(lane, F32)
    blk = 64

    def expsum(t, carry):
        for b in range(0, rows, blk):
            ref = mx[b:b + blk]
            acc = tg[b:b + blk]
            for k in range(tile // 128):
                acc = acc + jnp.exp(lg[b:b + blk, pl.ds(pl.multiple_of(t * tile + k * 128, 128), 128)] - ref)
            tg[b:b + blk] = acc
        return carry
    lax.fori_loop(0, tiles, expsum, 0)
    part_lse = top + jnp.log(jnp.sum(tg[...], axis=1, keepdims=True))
    groups = -(-rows // 128)
    st[...] = jnp.zeros(st.shape, F32)
    for i, piece in enumerate(lanes_of(jnp.broadcast_to(part_lse, lane))):
        st[i:i + 1, :] = piece
    for i, piece in enumerate(lanes_of(jnp.broadcast_to(hit, lane))):
        st[groups + i:groups + i + 1, :] = piece
    stats = [go(st, box.at[j], st_s.at[j], st_r.at[j], t) for j, t in enumerate(peers)]
    for cp in stats:
        cp.wait_recv()
    mine = st[...]
    best = jnp.maximum(mine, jnp.max(box[...], axis=0))
    total = jnp.exp(mine - best) + jnp.sum(jnp.exp(box[...] - best[None]), axis=0)
    lse = best + jnp.log(total)
    target = mine + jnp.sum(box[...], axis=0)
    count = live[0:1, :]
    missing = jnp.zeros((1, 128), F32)
    for i in range(groups):
        at = (lax.broadcasted_iota(jnp.int32, (1, 128), 1) + i * 128).astype(F32)
        missing = missing + jnp.where(at < count, lse[i:i + 1] - target[groups + i:groups + i + 1], 0.0)
    loss[...] = jnp.broadcast_to(jnp.sum(missing, axis=1, keepdims=True) / count, loss.shape)
    for i in range(groups):
        size = min(128, rows - i * 128)
        mx[i * 128:i * 128 + size] = jnp.broadcast_to(col_of(lse[i:i + 1], size), (size, 128))
    tg[...] = jnp.zeros(lane, F32)
    coef = scale_ref[0] / count

    def logit_grad(t, carry):
        for b in range(0, rows, blk):
            ref = mx[b:b + blk]
            factor = coef * meta[1, b:b + blk]
            want = meta[0, b:b + blk] - (offset + t * tile).astype(F32)
            acc = tg[b:b + blk]
            for k in range(tile // 128):
                cols = pl.ds(pl.multiple_of(t * tile + k * 128, 128), 128)
                l = lg[b:b + blk, cols]
                here = (lax.broadcasted_iota(jnp.int32, (1, 128), 1) + k * 128).astype(F32)
                hot = jnp.where((want == here) & (l > F_MIN), 1.0, 0.0)
                g = ((jnp.exp(l - ref) - hot) * factor).astype(BF16)
                gb[b:b + blk, cols] = g
                acc = acc + g.astype(F32) * l
            tg[b:b + blk] = acc
        return carry
    lax.fori_loop(0, tiles, logit_grad, 0)
    st2[...] = jnp.zeros(st2.shape, F32)
    for i, piece in enumerate(lanes_of(jnp.broadcast_to(jnp.sum(tg[...], axis=1, keepdims=True), lane))):
        st2[i:i + 1, :] = piece
    dots = [go(st2, box2.at[j], s2_s.at[j], s2_r.at[j], t) for j, t in enumerate(peers)]

    steps = width // (2 * tile)
    kb = tile // 128
    zrows = rows // nz
    mate = (x * 2 + (1 - core), v)
    spot = x * ny + y
    near = []
    for q in range(1, 4):
        tx, ty = flip(x, q // 2), flip(y, q % 2)
        near.append(((tx * 2 + core, z * ny + ty), tx * ny + ty))
    along = [(p, lax.rem(z + d, nz) * ny + y) for d in range(1, nz)]
    to_mate, to_near, to_z, ag_z, ag_x, ag_m = {}, {}, {}, {}, {}, {}

    def product(j, dst):
        acc = jnp.dot(gb[...], wv[:, pl.ds(pl.multiple_of(j * tile, tile), tile)],
                      preferred_element_type=F32)
        for k in range(kb):
            dst[k] = acc[:, k * 128:(k + 1) * 128]

    def for_mate(s):
        if s >= 2:
            to_mate[s - 2].wait_send()
        product(2 * s + (1 - core), ms.at[s % 2])
        to_mate[s] = remote(ms.at[s % 2], mr.at[s], m_s.at[s], m_r.at[s], mate)
        to_mate[s].start()

    def for_self(s):
        product(2 * s + core, ob)
        to_mate[s].wait_recv()
        for q, (target_id, block) in enumerate(near):
            sb[s, q] = (ob[block] + mr[s, block]).astype(BF16)
            to_near[s, q] = go(sb.at[s, q], rb.at[s, q], x_s.at[s, q], x_r.at[s, q], target_id)
        own[s] = ob[spot] + mr[s, spot]

    def plane(s):
        for q in range(3):
            to_near[s, q].wait_recv()
        own[s] = own[s] + (rb[s, 0].astype(F32) + rb[s, 1].astype(F32) + rb[s, 2].astype(F32))
        for d in range(1, nz):
            zz = lax.rem(z + d, nz)
            zs[s, d - 1] = own[s, pl.ds(pl.multiple_of(zz * zrows, 16), zrows)].astype(BF16)
            to_z[s, d] = go(zs.at[s, d - 1], zr.at[s, d - 1], z_s.at[s, d - 1], z_r.at[s, d - 1], along[d - 1])

    mine_rows = pl.ds(pl.multiple_of(z * zrows, 16), zrows)

    def row_dots():
        for cp in dots:
            cp.wait_recv()
        full = st2[...] + jnp.sum(box2[...], axis=0)
        for i in range(groups):
            size = min(128, rows - i * 128)
            tg[i * 128:i * 128 + size] = jnp.broadcast_to(col_of(full[i:i + 1], size), (size, 128))

    def finish(s):
        for d in range(1, nz):
            to_z[s, d].wait_recv()
        g = own[s, mine_rows]
        for d in range(1, nz):
            g = g + zr[s, d - 1].astype(F32)
        cols = pl.ds(pl.multiple_of((2 * s + core) * tile + spot * 128, 128), 128)
        r = meta[2, mine_rows]
        h = hc[mine_rows, cols].astype(F32)
        value = r * (gain[:, cols] * g) - (r * r) * h * (tg[mine_rows] * (1.0 / width))
        ag[core, spot, s, z] = value.astype(BF16)
        for d in range(1, nz):
            piece = ag.at[core, spot, s, z]
            ag_z[s, d] = go(piece, piece, az_s.at[s, d - 1], az_r.at[s, d - 1], along[d - 1])

    def spread(s):
        for d in range(1, nz):
            ag_z[s, d].wait_recv()
        piece = ag.at[core, spot, s]
        for q, (target_id, block) in enumerate(near):
            ag_x[s, q] = go(piece, piece, ax_s.at[s, q], ax_r.at[s, q], target_id)
        ag_m[s, 3] = go(piece, piece, am_s.at[s, 3], am_r.at[s, 3], mate)

    def share(s):
        for q, (target_id, block) in enumerate(near):
            ag_x[s, q].wait_recv()
            piece = ag.at[core, block, s]
            ag_m[s, q] = go(piece, piece, am_s.at[s, q], am_r.at[s, q], mate)

    def scatter(s):
        for q in range(4):
            ag_m[s, q].wait_recv()
        slots = out.shape[0]
        at = lax.broadcasted_iota(jnp.int32, (slots, rows), 1).astype(F32)
        back = jnp.where(at == jnp.broadcast_to(posn[p, :, 0:1], (slots, rows)), 1.0, 0.0).astype(BF16)
        for c in range(2):
            block = jnp.concatenate([ag[c, k, s].reshape(rows, 128) for k in range(kb)], axis=1)
            res = jnp.dot(back, block, preferred_element_type=F32).astype(BF16)
            out[:, (2 * s + c) * tile:(2 * s + c + 1) * tile] = res

    for s in range(steps):
        for_mate(s)
        if s >= 2:
            plane(s - 2)
        if s == 2:
            row_dots()
        if s >= 3:
            finish(s - 3)
        for_self(s)
    order = []
    for i in range(steps + 6):
        for lag, f in ((0, plane), (1, finish), (2, spread), (3, share), (4, scatter)):
            s = i + steps - 2 - lag
            if 0 <= s < steps and not (f is finish and s <= steps - 4):
                order.append((f, s))
    for f, s in order:
        f(s)
    for s in range(max(steps - 2, 0), steps):
        to_mate[s].wait_send()
    for cp in copies:
        cp.wait_send()


def head(nc, hc, meta, posn, live, norm_gain, out_weight, loss_scale, pipe, vocab, ny, slots):
    rows, width = nc.shape
    words = out_weight.shape[0]
    padded = -(-words // 512) * 512
    nz = vocab // ny
    steps = width // 1024
    n = pipe * vocab - 1
    zrows = rows // nz
    dma = pltpu.SemaphoreType.DMA
    vm = pltpu.VMEM
    return pl.pallas_call(
        functools.partial(head_kernel, pipe, vocab, ny, words),
        out_shape=(
            jax.ShapeDtypeStruct((slots, width), BF16),
            jax.ShapeDtypeStruct((8, 128), F32),
        ),
        in_specs=[pl.BlockSpec(memory_space=pltpu.SMEM), pl.BlockSpec(memory_space=pl.ANY)] + [VMEM] * 6,
        out_specs=(VMEM, VMEM),
        scratch_shapes=[
            vm((padded, width), BF16),
            vm((rows, padded), F32),
            vm((rows, padded), BF16),
            vm((rows, 128), F32), vm((rows, 128), F32),
            vm((8, 128), F32), vm((n, 8, 128), F32),
            vm((8, 128), F32), vm((n, 8, 128), F32),
            vm((2, 4, rows, 128), F32),
            vm((4, rows, 128), F32),
            vm((steps, 4, rows, 128), F32),
            vm((steps, 3, rows, 128), BF16),
            vm((steps, 3, rows, 128), BF16),
            vm((steps, rows, 128), F32),
            vm((steps, nz - 1, zrows, 128), BF16),
            vm((steps, nz - 1, zrows, 128), BF16),
            vm((2, 4, steps, nz, zrows, 128), BF16),
            dma((padded // 512,)),
            dma((n,)), dma((n,)), dma((n,)), dma((n,)),
            dma((steps,)), dma((steps,)),
            dma((steps, 3)), dma((steps, 3)),
            dma((steps, nz - 1)), dma((steps, nz - 1)),
            dma((steps, nz - 1)), dma((steps, nz - 1)),
            dma((steps, 3)), dma((steps, 3)),
            dma((steps, 4)), dma((steps, 4)),
        ],
        compiler_params=pltpu.CompilerParams(
            collective_id=1, has_side_effects=True, vmem_limit_bytes=62 * 2**20
        ),
    )(loss_scale.reshape(1), out_weight, nc, hc, meta, posn, live, norm_gain.reshape(1, width))


def body(pipe, vocab, hidden, norm_gain, out_weight, targets, loss_mask, slot_position, counts, loss_scale):
    micro_slots = hidden.shape[1]
    model_width = hidden.shape[2]
    shard_words = out_weight.shape[0]
    ny = 2
    nz = vocab // ny
    fast = (pipe == 4 and vocab == 8 and micro_slots == 128 and model_width % 1024 == 0
            and shard_words % 8 == 0)
    own_ints = jnp.concatenate(
        [targets, loss_mask, slot_position, jnp.zeros((5, micro_slots), jnp.int32)], axis=0
    )
    if fast:
        hc, nc, meta, posn, live = gather(
            hidden.reshape(micro_slots, model_width), own_ints, counts,
            norm_gain.reshape(1, model_width), pipe, ny, 4, LIVE_SHARE * pipe)
        grad_out, loss = head(nc, hc, meta, posn, live, norm_gain, out_weight, loss_scale,
                              pipe, vocab, ny, micro_slots)
        return (loss[0, 0], grad_out.reshape(1, micro_slots, model_width))
    offset = lax.axis_index(("pipe", "vocab")) * shard_words
    own_rows = hidden.reshape(micro_slots, model_width).astype(F32)
    own_normed = rms_scale(own_rows, norm_gain).astype(BF16)
    all_normed = lax.all_gather(own_normed, "pipe", axis=0, tiled=True)
    all_ints = lax.all_gather(own_ints, "pipe", axis=0)
    rows_total = all_normed.shape[0]
    all_targets, all_masks, all_positions = (
        all_ints[:, k].reshape(rows_total) for k in range(3)
    )
    count_row = jnp.broadcast_to(counts[:, None], (counts.shape[0], micro_slots)).reshape(rows_total)
    inside = all_positions < count_row
    token_weight = jnp.where(inside & (all_masks == 1), 1.0, 0.0).astype(F32)
    weight_total = jnp.sum(token_weight)
    logits = lax.dot_general(
        all_normed, out_weight, (((1,), (1,)), ((), ())), preferred_element_type=F32
    )
    is_target = (
        jnp.arange(shard_words, dtype=jnp.int32)[None, :] == (all_targets - offset)[:, None]
    )
    local_target = jnp.sum(jnp.where(is_target, logits, 0.0), axis=1)
    local_top = jnp.max(logits, axis=1)
    row_top = lax.pmax(local_top, ("pipe", "vocab"))
    local_total = jnp.sum(jnp.exp(logits - row_top[:, None]), axis=1)
    exp_total, target_logit = lax.psum((local_total, local_target), ("pipe", "vocab"))
    log_total = row_top + jnp.log(exp_total)
    loss = jnp.sum(token_weight * (log_total - target_logit)) / weight_total
    token_coef = loss_scale * token_weight / weight_total
    logit_grad = (
        (jnp.exp(logits - log_total[:, None]) - is_target.astype(F32)) * token_coef[:, None]
    ).astype(BF16)
    work_grad = jnp.dot(logit_grad, out_weight, preferred_element_type=F32)
    grad_cube = work_grad.reshape(rows_total // micro_slots, micro_slots, model_width)
    micro_grad = lax.psum_scatter(grad_cube, "pipe", scatter_dimension=0, tiled=True)
    summed = lax.psum(micro_grad, "vocab")
    grad_out = pull_rows(own_rows, norm_gain, summed.reshape(micro_slots, model_width))
    return (loss, grad_out.reshape(1, micro_slots, model_width))


def solution(mesh):
    in_specs = (
        P("pipe", None, None),
        P(),
        P(("pipe", "vocab"), None),
        P("pipe", None),
        P("pipe", None),
        P("pipe", None),
        P(),
        P(),
    )
    out_specs = (P(), P("pipe", None, None))
    part = functools.partial(body, mesh.shape["pipe"], mesh.shape["vocab"])
    return jax.shard_map(part, mesh=mesh, in_specs=in_specs, out_specs=out_specs, check_vma=False)
```

time: 152 us -> 111 us (0.73)
  the two profiles are of different devices: /device:TPU:16 before, /device:TPU:1 now
where the time goes in v1:
time: 111 us
  Pallas kernels  97.6 us (88%)
  local copies, waits for them, and re-layouts  11.2 us (10%)
  between operations  1.32 us (1%)
    pallas_call x1, Pallas kernels, head(): pl.pallas_call(functools.partial(head_kernel, pipe, vocab, ny, words), ou...  70.3 us
    pallas_call x1, Pallas kernels, gather(): pl.pallas_call(functools.partial(gather_kernel, ny, chunks), out_shape=(j...  27.4 us
    unnamed x17, local copies, waits for them, and re-layouts  9.94 us

profile of v1, /device:TPU:1, one launch (start us, length us, event | category | flops | bytes accessed | tf_op | source)
XLA Modules:
  0.0 110.9 jit_solution(18366562639032770217)
XLA Ops:
  1.3 0.1 pad.3.clone
  1.4 0.8 add_add_fusion.ints
  2.1 0.0 copy-start.2
  2.1 1.2 %copy-done.2 = bf16[1,128,4096]{2,1,0:T(8,128)(2,1)S(1)} copy-done((bf16[1,128,4096]{2,1,0:T(8,128)(2,1)S(1)}, bf16[1,128,4096]{2,1,0:T(8,128)(2,1)}, u32[]{:S(2)}) %copy-start.2) | copy-done | bytes 1048600
  3.3 0.0 copy-start.5
  3.3 0.7 copy-done.5
  4.1 0.0 copy-start.7
  4.1 0.7 copy-done.7
  4.7 27.4 %shard_map.95 = (bf16[320,4096]{1,0:T(8,128)(2,1)S(1)}, bf16[320,4096]{1,0:T(8,128)(2,1)S(1)}, f32[3,320,128]{2,1,0:T(8,128)S(1)}, f32[4,128,128]{2,1,0:T(8,128)S(1)}, f32[8,128]{1,0:T(8,128)S(1)}) custom-call(s32[4]{0:T(128)S(1)} %copy-done.7, bf16[128,4096]{1,0:T(8,128)(2,1)S(1)} %bitcast.6, s32[8,128]{1,0:T(8,128)S(1)} %add_add_fusion.ints, ...), custom_call_target="tpu_custom_call" | custom-call | tf_op jit(solution)/shard_map/pallas_call | solution.py:174
  32.1 0.0 copy-start
  32.1 1.5 %copy-done = bf16[320,4096]{1,0:T(8,128)(2,1)} copy-done((bf16[320,4096]{1,0:T(8,128)(2,1)}, bf16[320,4096]{1,0:T(8,128)(2,1)S(1)}, u32[]{:S(2)}) %copy-start) | copy-done | bytes 2621464
  33.6 0.0 copy-start.1
  33.6 1.5 %copy-done.1 = bf16[320,4096]{1,0:T(8,128)(2,1)} copy-done((bf16[320,4096]{1,0:T(8,128)(2,1)}, bf16[320,4096]{1,0:T(8,128)(2,1)S(1)}, u32[]{:S(2)}) %copy-start.1) | copy-done | bytes 2621464
  35.1 0.0 copy-start.3
  35.1 0.8 copy-done.3
  35.9 0.0 copy-start.4
  35.9 0.7 copy-done.4
  36.6 0.0 copy-start.6
  36.6 0.6 copy-done.6
  37.1 70.3 %shard_map.96 = (bf16[128,4096]{1,0:T(8,128)(2,1)}, f32[8,128]{1,0:T(8,128)}) custom-call(f32[1]{0:T(128)} %bitcast.5.scale_ref, bf16[4008,4096]{1,0:T(8,128)(2,1)} %weight.1, bf16[320,4096]{1,0:T(8,128)(2,1)} %copy-done.1, bf16[320,4096]{1,0:T(8,128)(2,1)} %copy-done, f32[3,320,128]{2,1,0:T(8,128)} %copy-done.3, f32[4,128,128]{2,1,0:T(8,128)} %copy-done.4, ...), custom_call_target="tpu_custom_call" | custom-call | tf_op jit(solution)/shard_map/pallas_call | solution.py:455
  107.4 1.2 %slice.3 = f32[1,1]{1,0:T(1,128)} slice(f32[8,128]{1,0:T(8,128)} %get-tuple-element.14), slice={[0:1], [0:1]} | slice | bytes 8 | tf_op jit(solution)/shard_map/slice | solution.py:511
  108.6 2.3 %copy.12 = bf16[1,128,4096]{2,1,0:T(8,128)(2,1)} copy(bf16[1,128,4096]{2,1,0:T(8,128)(2,1)} %bitcast.9) | data formatting | bytes 2097152
  (1 shorter events, 0.0 us)
Async XLA Ops:
  2.1 1.2 %copy-start.2 = (bf16[1,128,4096]{2,1,0:T(8,128)(2,1)S(1)}, bf16[1,128,4096]{2,1,0:T(8,128)(2,1)}, u32[]{:S(2)}) copy-start(bf16[1,128,4096]{2,1,0:T(8,128)(2,1)} %param.8) | copy-start | bytes 3145732
  3.3 0.7 copy-start.5
  4.1 0.7 copy-start.7
  32.1 1.5 %copy-start = (bf16[320,4096]{1,0:T(8,128)(2,1)}, bf16[320,4096]{1,0:T(8,128)(2,1)S(1)}, u32[]{:S(2)}) copy-start(bf16[320,4096]{1,0:T(8,128)(2,1)S(1)} %get-tuple-element.10.hc) | copy-start | bytes 7864324
  33.6 1.5 %copy-start.1 = (bf16[320,4096]{1,0:T(8,128)(2,1)}, bf16[320,4096]{1,0:T(8,128)(2,1)S(1)}, u32[]{:S(2)}) copy-start(bf16[320,4096]{1,0:T(8,128)(2,1)S(1)} %get-tuple-element.9.nc) | copy-start | bytes 7864324
  35.1 0.8 copy-start.3
  35.9 0.7 copy-start.4
  36.6 0.6 copy-start.6

commit v2 on v1

v2 whole, which is shorter than its diff:
```python
import functools
import jax
import jax.numpy as jnp
from jax import lax
from jax.experimental import pallas as pl
from jax.experimental.pallas import tpu as pltpu
from jax.sharding import PartitionSpec as P

EPSILON = 1e-05
MESH = pl.DeviceIdType.MESH
F32 = jnp.float32
BF16 = jnp.bfloat16
VMEM = pl.BlockSpec(memory_space=pltpu.VMEM)


def rms_scale(values, norm_gain):
    mean_square = jnp.mean(values * values, axis=-1, keepdims=True)
    return values * lax.rsqrt(mean_square + EPSILON) * norm_gain


def pull_rows(rows, norm_gain, cotangent):
    pullback = jax.vjp(lambda values: rms_scale(values, norm_gain), rows)[1]
    return pullback(cotangent)[0].astype(BF16)


def place(ny):
    p, v = lax.axis_index("pipe"), lax.axis_index("vocab")
    return p // 2, p % 2, v % ny, v // ny


def greet(targets):
    barrier = pltpu.get_barrier_semaphore()
    for target in targets:
        pl.semaphore_signal(barrier, inc=1, device_id=target, device_id_type=MESH)
    pl.semaphore_wait(barrier, len(targets))


def remote(src, dst, send, recv, target):
    return pltpu.make_async_remote_copy(
        src_ref=src, dst_ref=dst, send_sem=send, recv_sem=recv,
        device_id=target, device_id_type=MESH,
    )


LIVE_SHARE = 80
F_MIN = -1e30


def flip(i, by):
    return i + by * (1 - 2 * i)


def lanes_of(col):
    rows, lanes = col.shape
    outs = []
    for b in range(0, rows, lanes):
        part = col[b:min(b + lanes, rows)]
        r = lax.broadcasted_iota(jnp.int32, part.shape, 0)
        l = lax.broadcasted_iota(jnp.int32, part.shape, 1)
        outs.append(jnp.sum(jnp.where(r == l, part, 0.0), axis=0, keepdims=True))
    return outs


def col_of(row, count):
    shape = (count, row.shape[1])
    r = lax.broadcasted_iota(jnp.int32, shape, 0)
    l = lax.broadcasted_iota(jnp.int32, shape, 1)
    return jnp.sum(jnp.where(r == l, jnp.broadcast_to(row, shape), 0.0), axis=1, keepdims=True)


def head_kernel(pipe, vocab, ny, words, counts, scale_ref, hidden, targets, masks, places, gain_hbm, weight,
                out, loss, wv, lg, buf, sel, back, ti, gain, meta, live, hsel, mx, tg, sm,
                st, box, st2, box2, mr, sb, rb, own, zs, zr, ag,
                w_sem, o_sem, i_sem, f_s, f_r, n_s, n_r, c_s, c_r, d_s, d_r, e_s, e_r, t_s, t_r,
                st_s, st_r, s2_s, s2_r, m_s, m_r, x_s, x_r, z_s, z_r, az_s, az_r,
                ax_s, ax_r, am_s, am_r):
    x, core, y, z = place(ny)
    p, v = x * 2 + core, z * ny + y
    nz = vocab // ny
    slots, width = hidden.shape
    half = slots // 2
    rows = buf.shape[0]
    padded = wv.shape[0]
    tile = 512
    tiles = padded // tile
    rest = words - (tiles - 1) * tile
    lane = (rows, 128)
    offset = (p * vocab + v) * words
    chunks = width // tile
    far = 1 - x
    mate = (x * 2 + (1 - core), v)
    across = ((1 - x) * 2 + core, v)
    diag = ((1 - x) * 2 + (1 - core), v)
    beside = (p, z * ny + (1 - y))
    copies = []

    def go(src, dst, send, recv, target):
        cp = remote(src, dst, send, recv, target)
        cp.start()
        copies.append(cp)
        return cp

    def cols_at(c):
        return pl.ds(c * tile, tile)

    pool = (tiles - 1) * tile

    def half_rows(a, side):
        return pl.ds(pl.multiple_of(pool + (a * 2 + core) * slots + side * half, half), half)

    def side_rows(a):
        return pl.ds(pl.multiple_of(pool + a * 2 * slots, slots), 2 * slots)

    all_rows = pl.ds(pl.multiple_of(pool + p * slots, slots), slots)
    bring = [pltpu.make_async_copy(hidden.at[:, cols_at(c)], wv.at[all_rows, cols_at(c)], o_sem.at[c])
             for c in range(chunks)]
    small = [pltpu.make_async_copy(src, ti.at[p, k], i_sem.at[k])
             for k, src in enumerate((targets, masks, places))]
    small.append(pltpu.make_async_copy(gain_hbm, gain, i_sem.at[3]))
    for cp in small + bring:
        cp.start()

    def load(t):
        size = tile if t < tiles - 1 else rest
        return pltpu.make_async_copy(
            weight.at[pl.ds(t * tile, size)], wv.at[pl.ds(t * tile, size)], w_sem.at[t])

    peers = []
    for dp in range(pipe):
        for dv in range(vocab):
            if dp or dv:
                peers.append((lax.rem(p + dp, pipe), lax.rem(v + dv, vocab)))
    greet(peers)

    for cp in small:
        cp.wait()
    info = [go(ti.at[p], ti.at[p], t_s.at[j], t_r.at[j], target)
            for j, target in enumerate((mate, across, diag))]
    first, nigh, cross, second, third = [], [], [], [], []
    for c in range(chunks):
        bring[c].wait()
        piece = wv.at[half_rows(x, y), cols_at(c)]
        first.append(go(piece, piece, f_s.at[c], f_r.at[c], across))
        piece = wv.at[all_rows, cols_at(c)]
        nigh.append(go(piece, piece, n_s.at[c], n_r.at[c], mate))
    for t in range(tiles - 1):
        load(t).start()
    for cp in info:
        cp.wait_recv()

    square = (slots, slots)
    r0 = lax.broadcasted_iota(jnp.int32, square, 0)
    l0 = lax.broadcasted_iota(jnp.int32, square, 1)
    ri = lax.broadcasted_iota(jnp.int32, (rows, slots), 0).astype(F32)
    li = lax.broadcasted_iota(jnp.int32, (slots, rows), 1).astype(F32)
    base = jnp.zeros((1, 1), F32)
    tgt = jnp.zeros((rows, 1), F32)
    for m in range(pipe):
        inside = ti[m, 2] < counts[m]
        alive = jnp.where(inside & (ti[m, 1] == 1), 1.0, 0.0).astype(F32)
        alive_sq = jnp.broadcast_to(alive, square)
        col_live = jnp.sum(jnp.where(r0 == l0, alive_sq, 0.0), axis=1, keepdims=True)
        pos_col = jnp.sum(jnp.where(l0 < r0, alive_sq, 0.0), axis=1, keepdims=True) + base
        pos_row = jnp.sum(jnp.where(r0 < l0, jnp.broadcast_to(col_live, square), 0.0), axis=0, keepdims=True) + base
        one = jnp.where((ri == jnp.broadcast_to(pos_row, ri.shape))
                        & (jnp.broadcast_to(alive, ri.shape) == 1.0), 1.0, 0.0)
        sel[m // 2, :, (m % 2) * slots:(m % 2 + 1) * slots] = one.astype(BF16)
        tgt = tgt + jnp.sum(one * ti[m, 0].astype(F32), axis=1, keepdims=True)
        spots = jnp.where(col_live == 1.0, pos_col, -1.0)
        back[m] = jnp.where(li == jnp.broadcast_to(spots, li.shape), 1.0, 0.0).astype(BF16)
        base = base + jnp.sum(alive, axis=1, keepdims=True)
    live[...] = jnp.broadcast_to(base, live.shape)
    word = tgt - offset.astype(F32)
    meta[0] = jnp.broadcast_to(jnp.where((word >= 0.0) & (word < words), word, -1.0), lane)
    rl = lax.broadcasted_iota(jnp.int32, lane, 0).astype(F32)
    meta[1] = jnp.where(rl < jnp.broadcast_to(base, lane), 1.0, 0.0)
    sm[...] = jnp.zeros(lane, F32)

    def pass_on(c):
        first[c].wait_recv()
        piece = wv.at[half_rows(far, y), cols_at(c)]
        second.append(go(piece, piece, c_s.at[c], c_r.at[c], beside))
        cross.append(go(piece, piece, d_s.at[c], d_r.at[c], mate))

    def near_rows(c):
        nigh[c].wait_recv()
        buf[:, cols_at(c)] = jnp.dot(sel[x], wv[side_rows(x), cols_at(c)], preferred_element_type=F32).astype(BF16)

    def pass_mate(c):
        second[c].wait_recv()
        piece = wv.at[half_rows(far, 1 - y), cols_at(c)]
        third.append(go(piece, piece, e_s.at[c], e_r.at[c], mate))

    def far_rows(c):
        cross[c].wait_recv()
        third[c].wait_recv()
        h = jnp.dot(sel[far], wv[side_rows(far), cols_at(c)], preferred_element_type=F32)
        acc = sm[...]
        for k in range(tile // 128):
            at = c * tile + k * 128
            part = h[:, k * 128:(k + 1) * 128] + buf[:, at:at + 128].astype(F32)
            buf[:, at:at + 128] = part.astype(BF16)
            acc = acc + part * part
        sm[...] = acc

    for i in range(chunks + 3):
        for lag, f in ((0, pass_on), (0, near_rows), (2, pass_mate), (3, far_rows)):
            if 0 <= i - lag < chunks:
                f(i - lag)

    for cp in copies:
        cp.wait_send()
    copies.clear()
    edge = words // 16 * 16
    wv[edge:, :] = jnp.zeros((padded - edge, width), BF16)
    load(tiles - 1).start()
    mean = jnp.sum(sm[...], axis=1, keepdims=True) / width
    meta[2] = jnp.broadcast_to(lax.rsqrt(mean + EPSILON), lane)
    steps = width // (2 * tile)
    kb = tile // 128
    zrows = rows // nz
    spot = x * ny + y
    mine_rows = pl.ds(pl.multiple_of(z * zrows, 16), zrows)
    for s in range(steps):
        hsel[s] = buf[mine_rows, pl.ds(pl.multiple_of((2 * s + core) * tile + spot * 128, 128), 128)]

    def norm(c, carry):
        for k in range(tile // 128):
            cols = pl.ds(pl.multiple_of(c * tile + k * 128, 128), 128)
            buf[:, cols] = (buf[:, cols].astype(F32) * meta[2] * gain[:, cols]).astype(BF16)
        return carry
    lax.fori_loop(0, width // tile, norm, 0)

    mx[...] = jnp.full(lane, F_MIN, F32)
    tg[...] = jnp.zeros(lane, F32)
    sm[...] = jnp.zeros(lane, F32)

    def fold(t):
        for b in range(0, rows, 32):
            band = slice(b, b + 32)
            want = meta[0, band] - float(t * tile)
            old = mx[band]
            parts = [lg[band, t * tile + k * 128:t * tile + (k + 1) * 128] for k in range(tile // 128)]
            top = old
            for part in parts:
                top = jnp.maximum(top, part)
            hit = tg[band]
            acc = sm[band] * jnp.exp(old - top)
            for k, part in enumerate(parts):
                here = (lax.broadcasted_iota(jnp.int32, (1, 128), 1) + k * 128).astype(F32)
                hit = hit + jnp.where(want == here, part, 0.0)
                acc = acc + jnp.exp(part - top)
            mx[band] = top
            tg[band] = hit
            sm[band] = acc

    def multiply(t):
        wt = wv[t * tile:(t + 1) * tile, :]
        logit = lax.dot_general(buf[...], wt, (((1,), (1,)), ((), ())), preferred_element_type=F32)
        col = lax.broadcasted_iota(jnp.int32, (1, 128), 1)
        for k in range(tile // 128):
            part = logit[:, k * 128:(k + 1) * 128]
            first_word = t * tile + k * 128
            if first_word + 128 > words:
                part = jnp.where(col + first_word < words, part, F_MIN)
            lg[:, first_word:first_word + 128] = part

    for t in range(tiles):
        load(t).wait()
        if t:
            fold(t - 1)
        multiply(t)
    fold(tiles - 1)

    top = jnp.max(mx[...], axis=1, keepdims=True)
    hit = jnp.sum(tg[...], axis=1, keepdims=True)
    total = jnp.sum(sm[...] * jnp.exp(mx[...] - jnp.broadcast_to(top, lane)), axis=1, keepdims=True)
    part_lse = top + jnp.log(total)
    blk = 64
    groups = -(-rows // 128)
    st[...] = jnp.zeros(st.shape, F32)
    for i, piece in enumerate(lanes_of(jnp.broadcast_to(part_lse, lane))):
        st[i:i + 1, :] = piece
    stats = [go(st, box.at[j], st_s.at[j], st_r.at[j], t) for j, t in enumerate(peers)]
    st2[...] = jnp.zeros(st2.shape, F32)
    for i, piece in enumerate(lanes_of(jnp.broadcast_to(hit, lane))):
        st2[groups + i:groups + i + 1, :] = piece
    for cp in stats:
        cp.wait_recv()
    mine = st[...]
    best = jnp.maximum(mine, jnp.max(box[...], axis=0))
    total = jnp.exp(mine - best) + jnp.sum(jnp.exp(box[...] - best[None]), axis=0)
    lse = best + jnp.log(total)
    count = live[0:1, :]
    for i in range(groups):
        size = min(128, rows - i * 128)
        mx[i * 128:i * 128 + size] = jnp.broadcast_to(col_of(lse[i:i + 1], size), (size, 128))
    tg[...] = jnp.zeros(lane, F32)
    coef = scale_ref[0] / count

    def logit_grad(t, carry):
        for b in range(0, rows, blk):
            ref = mx[b:b + blk]
            factor = coef * meta[1, b:b + blk]
            want = meta[0, b:b + blk] - (t * tile).astype(F32)
            acc = tg[b:b + blk]
            for k in range(tile // 128):
                cols = pl.ds(pl.multiple_of(t * tile + k * 128, 128), 128)
                l = lg[b:b + blk, cols]
                here = (lax.broadcasted_iota(jnp.int32, (1, 128), 1) + k * 128).astype(F32)
                hot = jnp.where(want == here, 1.0, 0.0)
                g = ((jnp.exp(l - ref) - hot) * factor).astype(BF16)
                buf[b:b + blk, cols] = g
                acc = acc + g.astype(F32) * l
            tg[b:b + blk] = acc
        return carry
    lax.fori_loop(0, tiles, logit_grad, 0)
    for i, piece in enumerate(lanes_of(jnp.broadcast_to(jnp.sum(tg[...], axis=1, keepdims=True), lane))):
        st2[i:i + 1, :] = piece
    dots = [go(st2, box2.at[j], s2_s.at[j], s2_r.at[j], t) for j, t in enumerate(peers)]

    def ways(s):
        par = lax.rem(core + s, 2)
        found = []
        for a, b in ((1 - par, par), (par, 1 - par), (1, 1)):
            tx, ty = flip(x, a), flip(y, b)
            found.append(((tx * 2 + core, z * ny + ty), tx * ny + ty))
        return found
    along = [(p, lax.rem(z + d, nz) * ny + y) for d in range(1, nz)]
    to_mate, to_near, to_z, ag_z, ag_x, ag_m = {}, {}, {}, {}, {}, {}

    def product(j, slot):
        lg[:, slot * tile:(slot + 1) * tile] = jnp.dot(
            buf[:, :padded], wv[:, pl.ds(pl.multiple_of(j * tile, tile), tile)],
            preferred_element_type=F32)

    def for_mate(s):
        slot = 1 + s % 2
        if s >= 2:
            to_mate[s - 2].wait_send()
        product(2 * s + (1 - core), slot)
        to_mate[s] = remote(lg.at[:, slot * tile:(slot + 1) * tile], mr.at[s], m_s.at[s], m_r.at[s], mate)
        to_mate[s].start()

    def pair_sum(s, block):
        cols = pl.ds(pl.multiple_of(block * 128, 128), 128)
        return lg[:, cols] + mr[s, :, cols]

    def send_near(s, q, block, target):
        sb[s, q] = block.astype(BF16)
        to_near[s, q] = go(sb.at[s, q], rb.at[s, q], x_s.at[s, q], x_r.at[s, q], target)

    def for_self(s):
        product(2 * s + core, 0)
        to_mate[s].wait_recv()
        (one, b1), (two, b2), (opp, bd) = ways(s)
        send_near(s, 2, pair_sum(s, bd), opp)
        send_near(s, 0, pair_sum(s, b1), one)
        send_near(s, 1, pair_sum(s, b2), two)
        own[s] = pair_sum(s, spot)

    def plane(s):
        for q in range(3):
            to_near[s, q].wait_recv()
        own[s] = own[s] + (rb[s, 0].astype(F32) + rb[s, 1].astype(F32) + rb[s, 2].astype(F32))
        for d in range(1, nz):
            zz = lax.rem(z + d, nz)
            zs[s, d - 1] = own[s, pl.ds(pl.multiple_of(zz * zrows, 16), zrows)].astype(BF16)
            to_z[s, d] = go(zs.at[s, d - 1], zr.at[s, d - 1], z_s.at[s, d - 1], z_r.at[s, d - 1], along[d - 1])

    def row_dots():
        for cp in dots:
            cp.wait_recv()
        full = st2[...] + jnp.sum(box2[...], axis=0)
        missing = jnp.zeros((1, 128), F32)
        for i in range(groups):
            at = (lax.broadcasted_iota(jnp.int32, (1, 128), 1) + i * 128).astype(F32)
            missing = missing + jnp.where(at < count, lse[i:i + 1] - full[groups + i:groups + i + 1], 0.0)
        loss[0, 0] = jnp.sum(missing / count)
        for i in range(groups):
            size = min(128, rows - i * 128)
            tg[i * 128:i * 128 + size] = jnp.broadcast_to(col_of(full[i:i + 1], size), (size, 128))

    def finish(s):
        for d in range(1, nz):
            to_z[s, d].wait_recv()
        g = own[s, mine_rows]
        for d in range(1, nz):
            g = g + zr[s, d - 1].astype(F32)
        cols = pl.ds(pl.multiple_of((2 * s + core) * tile + spot * 128, 128), 128)
        r = meta[2, mine_rows]
        h = hsel[s].astype(F32)
        value = r * (gain[:, cols] * g) - (r * r) * h * (tg[mine_rows] * (1.0 / width))
        ag[core, spot, s, z] = value.astype(BF16)
        for d in range(1, nz):
            piece = ag.at[core, spot, s, z]
            ag_z[s, d] = go(piece, piece, az_s.at[s, d - 1], az_r.at[s, d - 1], along[d - 1])

    def send_plane(s, q, block, target):
        piece = ag.at[core, block, s]
        ag_x[s, q] = go(piece, piece, ax_s.at[s, q], ax_r.at[s, q], target)

    def send_mate(s, q, block):
        piece = ag.at[core, block, s]
        ag_m[s, q] = go(piece, piece, am_s.at[s, q], am_r.at[s, q], mate)

    def spread(s):
        for d in range(1, nz):
            ag_z[s, d].wait_recv()
        (one, b1), (two, b2), (opp, bd) = ways(s)
        send_plane(s, 0, spot, one)
        send_plane(s, 1, spot, two)
        send_plane(s, 2, spot, opp)
        send_mate(s, 3, spot)

    def share(s):
        for q, (target_id, block) in enumerate(ways(s)):
            ag_x[s, q].wait_recv()
            send_mate(s, q, block)

    def scatter(s):
        for q in range(4):
            ag_m[s, q].wait_recv()
        for c in range(2):
            block = jnp.concatenate([ag[c, k, s].reshape(rows, 128) for k in range(kb)], axis=1)
            res = jnp.dot(back[p], block, preferred_element_type=F32).astype(BF16)
            out[:, (2 * s + c) * tile:(2 * s + c + 1) * tile] = res

    for s in range(steps):
        for_mate(s)
        if s >= 3:
            plane(s - 3)
        for_self(s)
    row_dots()
    tail = []
    for i in range(steps + 6):
        for lag, f in ((0, plane), (1, finish), (2, spread), (3, share), (4, scatter)):
            s = i + steps - 3 - lag
            if 0 <= s < steps and not (f is plane and s <= steps - 4):
                tail.append((f, s))
    for f, s in tail:
        f(s)
    for s in range(max(steps - 2, 0), steps):
        to_mate[s].wait_send()
    for cp in copies:
        cp.wait_send()


def head(hidden, ints, norm_gain, out_weight, counts, loss_scale, pipe, vocab, ny):
    slots, width = hidden.shape
    rows = LIVE_SHARE * pipe
    words = out_weight.shape[0]
    padded = -(-words // 512) * 512
    nz = vocab // ny
    chunks = width // 512
    steps = width // 1024
    n = pipe * vocab - 1
    zrows = rows // nz
    dma = pltpu.SemaphoreType.DMA
    vm = pltpu.VMEM
    smem = pl.BlockSpec(memory_space=pltpu.SMEM)
    held = [pltpu.with_memory_space_constraint(a, pltpu.HBM)
            for a in (hidden, *ints, norm_gain.reshape(1, width), out_weight)]
    return pl.pallas_call(
        functools.partial(head_kernel, pipe, vocab, ny, words),
        out_shape=(
            jax.ShapeDtypeStruct((slots, width), BF16),
            jax.ShapeDtypeStruct((1, 1), F32),
        ),
        in_specs=[smem, smem] + [pl.BlockSpec(memory_space=pltpu.HBM)] * 6,
        out_specs=(VMEM, smem),
        scratch_shapes=[
            vm((padded, width), BF16),
            vm((rows, padded), F32),
            vm((rows, max(padded, width)), BF16),
            vm((2, rows, 2 * slots), BF16),
            vm((pipe, slots, rows), BF16),
            vm((pipe, 3, 1, slots), jnp.int32),
            vm((1, width), F32),
            vm((3, rows, 128), F32),
            vm((8, 128), F32),
            vm((steps, zrows, 128), BF16),
            vm((rows, 128), F32), vm((rows, 128), F32), vm((rows, 128), F32),
            vm((4, 128), F32), vm((n, 4, 128), F32),
            vm((8, 128), F32), vm((n, 8, 128), F32),
            vm((steps, rows, 512), F32),
            vm((steps, 3, rows, 128), BF16),
            vm((steps, 3, rows, 128), BF16),
            vm((steps, rows, 128), F32),
            vm((steps, nz - 1, zrows, 128), BF16),
            vm((steps, nz - 1, zrows, 128), BF16),
            vm((2, 4, steps, nz, zrows, 128), BF16),
            dma((padded // 512,)), dma((chunks,)), dma((4,)),
            dma((chunks,)), dma((chunks,)), dma((chunks,)), dma((chunks,)),
            dma((chunks,)), dma((chunks,)), dma((chunks,)), dma((chunks,)),
            dma((chunks,)), dma((chunks,)), dma((3,)), dma((3,)),
            dma((n,)), dma((n,)), dma((n,)), dma((n,)),
            dma((steps,)), dma((steps,)),
            dma((steps, 3)), dma((steps, 3)),
            dma((steps, nz - 1)), dma((steps, nz - 1)),
            dma((steps, nz - 1)), dma((steps, nz - 1)),
            dma((steps, 3)), dma((steps, 3)),
            dma((steps, 4)), dma((steps, 4)),
        ],
        compiler_params=pltpu.CompilerParams(
            collective_id=0, has_side_effects=True, vmem_limit_bytes=52 * 2**20
        ),
    )(counts, loss_scale.reshape(1), *held)


def body(pipe, vocab, hidden, norm_gain, out_weight, targets, loss_mask, slot_position, counts, loss_scale):
    micro_slots = hidden.shape[1]
    model_width = hidden.shape[2]
    shard_words = out_weight.shape[0]
    ny = 2
    nz = vocab // ny
    fast = (pipe == 4 and vocab == 8 and micro_slots == 128 and micro_slots * pipe == 512 and model_width % 1024 == 0
            and shard_words % 8 == 0)
    if fast:
        grad_out, loss = head(
            hidden.reshape(micro_slots, model_width), (targets, loss_mask, slot_position),
            norm_gain, out_weight, counts, loss_scale, pipe, vocab, ny)
        return (loss[0, 0], grad_out.reshape(1, micro_slots, model_width))
    own_ints = jnp.concatenate(
        [targets, loss_mask, slot_position, jnp.zeros((5, micro_slots), jnp.int32)], axis=0
    )
    offset = lax.axis_index(("pipe", "vocab")) * shard_words
    own_rows = hidden.reshape(micro_slots, model_width).astype(F32)
    own_normed = rms_scale(own_rows, norm_gain).astype(BF16)
    all_normed = lax.all_gather(own_normed, "pipe", axis=0, tiled=True)
    all_ints = lax.all_gather(own_ints, "pipe", axis=0)
    rows_total = all_normed.shape[0]
    all_targets, all_masks, all_positions = (
        all_ints[:, k].reshape(rows_total) for k in range(3)
    )
    count_row = jnp.broadcast_to(counts[:, None], (counts.shape[0], micro_slots)).reshape(rows_total)
    inside = all_positions < count_row
    token_weight = jnp.where(inside & (all_masks == 1), 1.0, 0.0).astype(F32)
    weight_total = jnp.sum(token_weight)
    logits = lax.dot_general(
        all_normed, out_weight, (((1,), (1,)), ((), ())), preferred_element_type=F32
    )
    is_target = (
        jnp.arange(shard_words, dtype=jnp.int32)[None, :] == (all_targets - offset)[:, None]
    )
    local_target = jnp.sum(jnp.where(is_target, logits, 0.0), axis=1)
    local_top = jnp.max(logits, axis=1)
    row_top = lax.pmax(local_top, ("pipe", "vocab"))
    local_total = jnp.sum(jnp.exp(logits - row_top[:, None]), axis=1)
    exp_total, target_logit = lax.psum((local_total, local_target), ("pipe", "vocab"))
    log_total = row_top + jnp.log(exp_total)
    loss = jnp.sum(token_weight * (log_total - target_logit)) / weight_total
    token_coef = loss_scale * token_weight / weight_total
    logit_grad = (
        (jnp.exp(logits - log_total[:, None]) - is_target.astype(F32)) * token_coef[:, None]
    ).astype(BF16)
    work_grad = jnp.dot(logit_grad, out_weight, preferred_element_type=F32)
    grad_cube = work_grad.reshape(rows_total // micro_slots, micro_slots, model_width)
    micro_grad = lax.psum_scatter(grad_cube, "pipe", scatter_dimension=0, tiled=True)
    summed = lax.psum(micro_grad, "vocab")
    grad_out = pull_rows(own_rows, norm_gain, summed.reshape(micro_slots, model_width))
    return (loss, grad_out.reshape(1, micro_slots, model_width))


def solution(mesh):
    in_specs = (
        P("pipe", None, None),
        P(),
        P(("pipe", "vocab"), None),
        P("pipe", None),
        P("pipe", None),
        P("pipe", None),
        P(),
        P(),
    )
    out_specs = (P(), P("pipe", None, None))
    part = functools.partial(body, mesh.shape["pipe"], mesh.shape["vocab"])
    return jax.shard_map(part, mesh=mesh, in_specs=in_specs, out_specs=out_specs, check_vma=False)
```

time: 111 us -> 96.7 us (0.87)
  local copies, waits for them, and re-layouts: 11.2 us -> 1.62 us
  Pallas kernels: 97.6 us -> 91.9 us
  between operations: 1.32 us -> 3.06 us
    pallas_call x1 -> x0, Pallas kernels: 27.4 us -> none  [gather(): pl.pallas_call(functools.partial(gather_kernel, ny, chunks), out_shape=(j...]
    pallas_call x1, Pallas kernels: 70.3 us -> 91.9 us  [head(): pl.pallas_call(functools.partial(head_kernel, pipe, vocab, ny, words), ou...]
    unnamed x17 -> x3, local copies, waits for them, and re-layouts: 9.94 us -> 1.62 us
    slice x1 -> x0, local copies, waits for them, and re-layouts: 1.19 us -> none  [body(): return (loss[0, 0], grad_out.reshape(1, micro_slots, model_width))]
where the time goes in v2:
time: 96.7 us; the launch traced here: 96.5 us
  Pallas kernels  91.9 us (95%)
  between operations  3.06 us (3%)
  local copies, waits for them, and re-layouts  1.62 us (2%)
    pallas_call x1, Pallas kernels, head(): pl.pallas_call(functools.partial(head_kernel, pipe, vocab, ny, words), ou...  91.9 us

profile of v2, /device:TPU:1, one launch (start us, length us, event | category | flops | bytes accessed | tf_op | source)
XLA Modules:
  0.0 96.5 jit_solution(13478321065905172830)
XLA Ops:
  1.3 0.0 copy-start
  1.3 0.6 copy-done
  1.9 91.9 %shard_map.95 = (bf16[128,4096]{1,0:T(8,128)(2,1)S(1)}, f32[1,1]{1,0:T(1,128)}) custom-call(s32[4]{0:T(128)S(1)} %copy-done, f32[1]{0:T(128)} %bitcast.5.scale_ref, bf16[128,4096]{1,0:T(8,128)(2,1)} %bitcast.7, s32[1,128]{1,0:T(1,128)} %targets.1, s32[1,128]{1,0:T(1,128)} %masks.1, s32[1,128]{1,0:T(1,128)} %places.1, f32[1,4096]{1,0:T(1,128)} %bitcast.8, ...), custom_call_target="tpu_custom_call" | custom-call | tf_op jit(solution)/shard_map/pallas_call | solution.py:464
  94.4 1.0 %copy.14 = bf16[1,128,4096]{2,1,0:T(8,128)(2,1)} copy(bf16[1,128,4096]{2,1,0:T(8,128)(2,1)S(1)} %bitcast.6) | data formatting | bytes 2097152
Async XLA Ops:
  1.3 0.7 copy-start

commit v3 on v2

--- a/solution.py
+++ b/solution.py
@@ -71,7 +71,7 @@
 def head_kernel(pipe, vocab, ny, words, counts, scale_ref, hidden, targets, masks, places, gain_hbm, weight,
                 out, loss, wv, lg, buf, sel, back, ti, gain, meta, live, hsel, mx, tg, sm,
                 st, box, st2, box2, mr, sb, rb, own, zs, zr, ag,
-                w_sem, o_sem, i_sem, f_s, f_r, n_s, n_r, c_s, c_r, d_s, d_r, e_s, e_r, t_s, t_r,
+                ready, w_sem, o_sem, i_sem, f_s, f_r, n_s, n_r, c_s, c_r, d_s, d_r, e_s, e_r, t_s, t_r,
                 st_s, st_r, s2_s, s2_r, m_s, m_r, x_s, x_r, z_s, z_r, az_s, az_r,
                 ax_s, ax_r, am_s, am_r):
     x, core, y, z = place(ny)
@@ -130,7 +130,26 @@
         for dv in range(vocab):
             if dp or dv:
                 peers.append((lax.rem(p + dp, pipe), lax.rem(v + dv, vocab)))
-    greet(peers)
+    close = [mate, across, diag, beside]
+    inner = (z > 0).astype(jnp.int32) + (z < nz - 1).astype(jnp.int32)
+
+    def call_column(sem):
+        @pl.when(z > 0)
+        def _():
+            pl.semaphore_signal(sem, inc=1, device_id=(p, v - ny), device_id_type=MESH)
+
+        @pl.when(z < nz - 1)
+        def _():
+            pl.semaphore_signal(sem, inc=1, device_id=(p, v + ny), device_id_type=MESH)
+
+    def call_close(sem):
+        for target in close:
+            pl.semaphore_signal(sem, inc=1, device_id=target, device_id_type=MESH)
+
+    entry = pltpu.get_barrier_semaphore()
+    call_close(entry)
+    call_column(entry)
+    pl.semaphore_wait(entry, inner + len(close))
 
     for cp in small:
         cp.wait()
@@ -145,6 +164,9 @@
         nigh.append(go(piece, piece, n_s.at[c], n_r.at[c], mate))
     for t in range(tiles - 1):
         load(t).start()
+    call_column(ready.at[0])
+    pl.semaphore_wait(ready.at[0], inner)
+    call_column(ready.at[1])
     for cp in info:
         cp.wait_recv()
 
@@ -170,6 +192,8 @@
         back[m] = jnp.where(li == jnp.broadcast_to(spots, li.shape), 1.0, 0.0).astype(BF16)
         base = base + jnp.sum(alive, axis=1, keepdims=True)
     live[...] = jnp.broadcast_to(base, live.shape)
+    pl.semaphore_wait(ready.at[1], inner)
+    call_close(ready.at[2])
     word = tgt - offset.astype(F32)
     meta[0] = jnp.broadcast_to(jnp.where((word >= 0.0) & (word < words), word, -1.0), lane)
     rl = lax.broadcasted_iota(jnp.int32, lane, 0).astype(F32)
@@ -204,6 +228,11 @@
         sm[...] = acc
 
     for i in range(chunks + 3):
+        if i == 3:
+            pl.semaphore_wait(ready.at[2], len(close))
+            call_close(ready.at[3])
+        if i == 6:
+            pl.semaphore_wait(ready.at[3], len(close))
         for lag, f in ((0, pass_on), (0, near_rows), (2, pass_mate), (3, far_rows)):
             if 0 <= i - lag < chunks:
                 f(i - lag)
@@ -490,7 +519,7 @@
             vm((steps, nz - 1, zrows, 128), BF16),
             vm((steps, nz - 1, zrows, 128), BF16),
             vm((2, 4, steps, nz, zrows, 128), BF16),
-            dma((padded // 512,)), dma((chunks,)), dma((4,)),
+            pltpu.SemaphoreType.REGULAR((4,)), dma((padded // 512,)), dma((chunks,)), dma((4,)),
             dma((chunks,)), dma((chunks,)), dma((chunks,)), dma((chunks,)),
             dma((chunks,)), dma((chunks,)), dma((chunks,)), dma((chunks,)),
             dma((chunks,)), dma((chunks,)), dma((3,)), dma((3,)),

time: 96.7 us -> 94 us (0.972)
  Pallas kernels: 91.9 us -> 89.2 us
    pallas_call x1, Pallas kernels: 91.9 us -> 89.2 us  [head(): pl.pallas_call(functools.partial(head_kernel, pipe, vocab, ny, words), ou...]
where the time goes in v3:
time: 94 us; the launch traced here: 93.9 us
  Pallas kernels  89.2 us (95%)
  between operations  3.06 us (3%)
  local copies, waits for them, and re-layouts  1.62 us (2%)
    pallas_call x1, Pallas kernels, head(): pl.pallas_call(functools.partial(head_kernel, pipe, vocab, ny, words), ou...  89.2 us

profile of v3, /device:TPU:1, one launch (start us, length us, event | category | flops | bytes accessed | tf_op | source)
XLA Modules:
  0.0 93.9 jit_solution(5952567681635365175)
XLA Ops:
  1.3 0.0 copy-start
  1.3 0.6 copy-done
  1.9 89.2 %shard_map.95 = (bf16[128,4096]{1,0:T(8,128)(2,1)S(1)}, f32[1,1]{1,0:T(1,128)}) custom-call(s32[4]{0:T(128)S(1)} %copy-done, f32[1]{0:T(128)} %bitcast.5.scale_ref, bf16[128,4096]{1,0:T(8,128)(2,1)} %bitcast.7, s32[1,128]{1,0:T(1,128)} %targets.1, s32[1,128]{1,0:T(1,128)} %masks.1, s32[1,128]{1,0:T(1,128)} %places.1, f32[1,4096]{1,0:T(1,128)} %bitcast.8, ...), custom_call_target="tpu_custom_call" | custom-call | tf_op jit(solution)/shard_map/pallas_call | solution.py:493
  91.8 1.0 %copy.14 = bf16[1,128,4096]{2,1,0:T(8,128)(2,1)} copy(bf16[1,128,4096]{2,1,0:T(8,128)(2,1)S(1)} %bitcast.6) | data formatting | bytes 2097152
Async XLA Ops:
  1.3 0.7 copy-start
